TPU v7x, 32 devices: a 4x4x1 block of a 4x4x8 slice. The times are simulated.
32 devices in a mesh: batch: 1 (over z), cols: 4 (over y), rows: 8 (over x, core).
Axes of the slice: x: 4, y: 4, z: 1, core: 2. Of those that a mesh axis runs over, the one named last changes fastest.
The devices are a block of a 4x4x8 slice.
Arguments:
- frames: bfloat16 [4, 2, 64, 96, 256], P(None, 'batch', 'rows', 'cols')
- w_x: bfloat16 [3, 3, 256, 1536], replicated
- w_h: bfloat16 [3, 3, 384, 1536], replicated
- gate_bias: float32 [1536], replicated
- h_init: bfloat16 [2, 64, 96, 384], P('batch', 'rows', 'cols')
- c_init: float32 [2, 64, 96, 384], P('batch', 'rows', 'cols')
Outputs:
- output 1: bfloat16 [4, 2, 64, 96, 384], P(None, 'batch', 'rows', 'cols')
- output 2: float32 [2, 64, 96, 384], P('batch', 'rows', 'cols')
All inputs are finite; a program needn't handle non-finite values.
Results may differ from a plain program's by a relative error of at most 0.001.
Values are sent between devices in bfloat16 or wider.
A program may use at most 768 MiB of HBM per device.

v0:
```python
import jax
import jax.numpy as jnp
from jax import lax
from jax.sharding import PartitionSpec as P, NamedSharding


def edge_swap(tile_arr, halo_width, split_dim, axis_label, axis_count):
    length = tile_arr.shape[split_dim]
    low_edge = lax.slice_in_dim(tile_arr, 0, halo_width, axis=split_dim)
    high_edge = lax.slice_in_dim(tile_arr, length - halo_width, length, axis=split_dim)
    down_pairs = [(source, source + 1) for source in range(axis_count - 1)]
    up_pairs = [(source + 1, source) for source in range(axis_count - 1)]
    from_prev = lax.ppermute(high_edge, axis_label, down_pairs)
    from_next = lax.ppermute(low_edge, axis_label, up_pairs)
    return jnp.concatenate([from_prev, tile_arr, from_next], axis=split_dim)


def with_halo(tile_arr, halo_width, row_dim, row_count, col_count):
    row_ext = edge_swap(tile_arr, halo_width, row_dim, "rows", row_count)
    return edge_swap(row_ext, halo_width, row_dim + 1, "cols", col_count)


def conv_taps(padded, weights, out_rows, out_cols):
    tap_list = [padded[:, row_off:row_off + out_rows, col_off:col_off + out_cols, :] for row_off in range(3) for col_off in range(3)]
    patches = jnp.concatenate(tap_list, axis=-1)
    flat_patches = patches.reshape(-1, patches.shape[-1])
    flat_weights = weights.reshape(-1, weights.shape[-1])
    product = jnp.dot(flat_patches, flat_weights, preferred_element_type=jnp.float32)
    return product.reshape(padded.shape[0], out_rows, out_cols, -1)


def lstm_cell(gate_sum, cell_prev):
    hidden_width = cell_prev.shape[-1]
    in_gate = jax.nn.sigmoid(gate_sum[..., :hidden_width])
    forget_gate = jax.nn.sigmoid(gate_sum[..., hidden_width:2 * hidden_width])
    out_gate = jax.nn.sigmoid(gate_sum[..., 2 * hidden_width:3 * hidden_width])
    cand_gate = jnp.tanh(gate_sum[..., 3 * hidden_width:])
    cell_next = forget_gate * cell_prev + in_gate * cand_gate
    hidden_next = (out_gate * jnp.tanh(cell_next)).astype(jnp.bfloat16)
    return hidden_next, cell_next


def solution(mesh):
    row_count = mesh.shape["rows"]
    col_count = mesh.shape["cols"]
    frame_spec = P(None, "batch", "rows", "cols", None)
    state_spec = P("batch", "rows", "cols", None)

    def local_run(frames, w_x, w_h, gate_bias, h_init, c_init):
        tile_rows = h_init.shape[1]
        tile_cols = h_init.shape[2]
        frames_ext = with_halo(frames, 1, 2, row_count, col_count)

        def step_fn(state_pair, frame_ext):
            hidden, cell_state = state_pair
            hidden_ext = with_halo(hidden, 1, 1, row_count, col_count)
            gate_sum = conv_taps(frame_ext, w_x, tile_rows, tile_cols) + conv_taps(hidden_ext, w_h, tile_rows, tile_cols) + gate_bias
            hidden_next, cell_next = lstm_cell(gate_sum, cell_state)
            return (hidden_next, cell_next), hidden_next

        final_pair, all_hidden = lax.scan(step_fn, (h_init, c_init), frames_ext)
        return all_hidden, final_pair[1]

    return jax.shard_map(local_run, mesh=mesh, in_specs=(frame_spec, P(), P(), P(), state_spec, state_spec), out_specs=(frame_spec, state_spec), check_vma=False)
```

profile of v0, /device:TPU:97, one launch (start us, length us, event | category | flops | bytes accessed | tf_op | source)
XLA Modules:
  0.0 157.3 jit_solution(4401831135058435838)
XLA Ops:
  1.7 4.6 %collective-permute-start.4 = (bf16[4,2,1,24,256]{4,3,2,1,0:T(8,128)(2,1)S(1)}, bf16[4,2,1,24,256]{4,3,2,1,0:T(8,128)(2,1)S(1)}, u32[]{:S(2)}, u32[]{:S(2)}) collective-permute-start(bf16[4,2,1,24,256]{4,3,2,1,0:T(8,128)(2,1)S(1)} %get-tuple-element.73), channel_id=1, source_target_pairs={{0,1},{1,2},{2,3},{3,4},{4,5},{5,6},{6,7},{8,9},{9,10},{10,11},{11... | collective-permute-start | bytes 294920 | tf_op jit(solution)/shard_map/ppermute | solution.py:13
  8.5 3.9 %collective-permute-done.5 = bf16[4,2,1,24,256]{4,3,2,1,0:T(8,128)(2,1)S(1)} collective-permute-done((bf16[4,2,1,24,256]{4,3,2,1,0:T(8,128)(2,1)S(1)}, bf16[4,2,1,24,256]{4,3,2,1,0:T(8,128)(2,1)S(1)}, u32[]{:S(2)}, u32[]{:S(2)}) %collective-permute-start.5) | collective-permute-done | bytes 98336 | tf_op jit(solution)/shard_map/ppermute | solution.py:14
  13.5 3.8 %collective-permute-start.6 = (bf16[4,2,10,1,256]{4,3,2,1,0:T(2,128)(2,1)S(1)}, bf16[4,2,10,1,256]{4,3,2,1,0:T(2,128)(2,1)S(1)}, u32[]{:S(2)}, u32[]{:S(2)}) collective-permute-start(bf16[4,2,10,1,256]{4,3,2,1,0:T(2,128)(2,1)S(1)} %get-tuple-element.70), channel_id=1, source_target_pairs={{0,8},{8,16},{16,24},{1,9},{9,17},{17,25},{2,10},{10,18},{18,26},{... | collective-permute-start | bytes 122888 | tf_op jit(solution)/shard_map/ppermute | solution.py:13
  18.8 4.1 %collective-permute-done.7 = bf16[4,2,10,1,256]{4,3,2,1,0:T(2,128)(2,1)S(1)} collective-permute-done((bf16[4,2,10,1,256]{4,3,2,1,0:T(2,128)(2,1)S(1)}, bf16[4,2,10,1,256]{4,3,2,1,0:T(2,128)(2,1)S(1)}, u32[]{:S(2)}, u32[]{:S(2)}) %collective-permute-start.7) | collective-permute-done | bytes 40992 | tf_op jit(solution)/shard_map/ppermute | solution.py:14
  25.0 131.5 %while.14 = (s32[]{:T(128)}, bf16[2,8,24,384]{3,2,1,0:T(8,128)(2,1)S(1)}, f32[2,8,24,384]{3,2,1,0:T(8,128)S(1)}, bf16[4,2,8,24,384]{4,3,2,1,0:T(8,128)(2,1)}, bf...) while((s32[]{:T(128)}, ...), condition=%wide.region_1.2_spmd, body=%wide.region_0.1_spmd.sunk | while | flops 6802735104 | bytes 54197544 | solution.py:61
  25.0 3.0 %collective-permute-start = (bf16[2,1,24,384]{3,2,1,0:T(8,128)(2,1)S(1)}, bf16[2,1,24,384]{3,2,1,0:T(8,128)(2,1)S(1)}, u32[]{:S(2)}, u32[]{:S(2)}) collective-permute-start(bf16[2,1,24,384]{3,2,1,0:T(8,128)(2,1)S(1)} %get-tuple-element.130), channel_id=1, source_target_pairs={{0,1},{1,2},{2,3},{3,4},{4,5},{5,6},{6,7},{8,9},{9,10},{10,11},{11... | collective-permute-start | bytes 110600 | tf_op jit(solution)/shard_map/while/body/eval_jaxpr/ppermute | solution.py:13
  30.7 2.6 %collective-permute-done.1 = bf16[2,1,24,384]{3,2,1,0:T(8,128)(2,1)S(1)} collective-permute-done((bf16[2,1,24,384]{3,2,1,0:T(8,128)(2,1)S(1)}, bf16[2,1,24,384]{3,2,1,0:T(8,128)(2,1)S(1)}, u32[]{:S(2)}, u32[]{:S(2)}) %collective-permute-start.1) | collective-permute-done | bytes 36896 | tf_op jit(solution)/shard_map/while/body/eval_jaxpr/ppermute | solution.py:14
  33.4 3.9 %collective-permute-start.2 = (bf16[2,10,1,384]{3,2,1,0:T(2,128)(2,1)S(1)}, bf16[2,10,1,384]{3,2,1,0:T(2,128)(2,1)S(1)}, u32[]{:S(2)}, u32[]{:S(2)}) collective-permute-start(bf16[2,10,1,384]{3,2,1,0:T(2,128)(2,1)S(1)} %get-tuple-element.132), channel_id=1, source_target_pairs={{0,8},{8,16},{16,24},{1,9},{9,17},{17,25},{2,10},{10,18},{18,26},{... | collective-permute-start | bytes 46088 | tf_op jit(solution)/shard_map/while/body/eval_jaxpr/ppermute | solution.py:13
  37.3 7.4 %fusion.58 = f32[2,8,24,1536]{3,2,1,0:T(8,128)} fusion(bf16[2,8,24,2304]{3,2,1,0:T(8,128)(2,1)S(1)} %slice_dynamic-update-slice_fusion.26, bf16[2304,1536,1,1]{1,0,3,2:T(8,128)(2,1)} %bitcast.35), kind=kOutput, calls=%fused_computation.67.clone.1 | convolution fusion | flops 2717908992 | bytes 11206656 | tf_op jit(solution)/shard_map/while/body/eval_jaxpr/dot_general | solution.py:28
  46.2 3.4 %collective-permute-done.3 = bf16[2,10,1,384]{3,2,1,0:T(2,128)(2,1)S(1)} collective-permute-done((bf16[2,10,1,384]{3,2,1,0:T(2,128)(2,1)S(1)}, bf16[2,10,1,384]{3,2,1,0:T(2,128)(2,1)S(1)}, u32[]{:S(2)}, u32[]{:S(2)}) %collective-permute-start.3) | collective-permute-done | bytes 15392 | tf_op jit(solution)/shard_map/while/body/eval_jaxpr/ppermute | solution.py:14
  50.3 7.3 %fusion.69 = f32[2,8,24,1536]{3,2,1,0:T(8,128)S(1)} fusion(f32[2,8,24,1536]{3,2,1,0:T(8,128)S(1)} %copy-done.6, bf16[2,8,24,3456]{3,2,1,0:T(8,128)(2,1)S(1)} %fusion.68, bf16[3456,1536,1,1]{1,0,3,2:T(8,128)(2,1)} %bitcast.34, f32[1536]{0:T(1024)S(1)} %get-tuple-element.162), kind=kOutput, calls=%fused_computation.1.clone.1 | convolution fusion | flops 4078043136 | bytes 17995776 | tf_op jit(solution)/shard_map/while/body/eval_jaxpr/dot_general | solution.py:28
  59.0 3.2 %collective-permute-start = (bf16[2,1,24,384]{3,2,1,0:T(8,128)(2,1)S(1)}, bf16[2,1,24,384]{3,2,1,0:T(8,128)(2,1)S(1)}, u32[]{:S(2)}, u32[]{:S(2)}) collective-permute-start(bf16[2,1,24,384]{3,2,1,0:T(8,128)(2,1)S(1)} %get-tuple-element.130), channel_id=1, source_target_pairs={{0,1},{1,2},{2,3},{3,4},{4,5},{5,6},{6,7},{8,9},{9,10},{10,11},{11... | collective-permute-start | bytes 110600 | tf_op jit(solution)/shard_map/while/body/eval_jaxpr/ppermute | solution.py:13
  67.6 3.6 %collective-permute-start.2 = (bf16[2,10,1,384]{3,2,1,0:T(2,128)(2,1)S(1)}, bf16[2,10,1,384]{3,2,1,0:T(2,128)(2,1)S(1)}, u32[]{:S(2)}, u32[]{:S(2)}) collective-permute-start(bf16[2,10,1,384]{3,2,1,0:T(2,128)(2,1)S(1)} %get-tuple-element.132), channel_id=1, source_target_pairs={{0,8},{8,16},{16,24},{1,9},{9,17},{17,25},{2,10},{10,18},{18,26},{... | collective-permute-start | bytes 46088 | tf_op jit(solution)/shard_map/while/body/eval_jaxpr/ppermute | solution.py:13
  71.1 7.4 %fusion.58 = f32[2,8,24,1536]{3,2,1,0:T(8,128)} fusion(bf16[2,8,24,2304]{3,2,1,0:T(8,128)(2,1)S(1)} %slice_dynamic-update-slice_fusion.26, bf16[2304,1536,1,1]{1,0,3,2:T(8,128)(2,1)} %bitcast.35), kind=kOutput, calls=%fused_computation.67.clone.1 | convolution fusion | flops 2717908992 | bytes 11206656 | tf_op jit(solution)/shard_map/while/body/eval_jaxpr/dot_general | solution.py:28
  80.0 3.2 %collective-permute-done.3 = bf16[2,10,1,384]{3,2,1,0:T(2,128)(2,1)S(1)} collective-permute-done((bf16[2,10,1,384]{3,2,1,0:T(2,128)(2,1)S(1)}, bf16[2,10,1,384]{3,2,1,0:T(2,128)(2,1)S(1)}, u32[]{:S(2)}, u32[]{:S(2)}) %collective-permute-start.3) | collective-permute-done | bytes 15392 | tf_op jit(solution)/shard_map/while/body/eval_jaxpr/ppermute | solution.py:14
  84.0 7.3 %fusion.69 = f32[2,8,24,1536]{3,2,1,0:T(8,128)S(1)} fusion(f32[2,8,24,1536]{3,2,1,0:T(8,128)S(1)} %copy-done.6, bf16[2,8,24,3456]{3,2,1,0:T(8,128)(2,1)S(1)} %fusion.68, bf16[3456,1536,1,1]{1,0,3,2:T(8,128)(2,1)} %bitcast.34, f32[1536]{0:T(1024)S(1)} %get-tuple-element.162), kind=kOutput, calls=%fused_computation.1.clone.1 | convolution fusion | flops 4078043136 | bytes 17995776 | tf_op jit(solution)/shard_map/while/body/eval_jaxpr/dot_general | solution.py:28
  92.6 3.4 %collective-permute-start = (bf16[2,1,24,384]{3,2,1,0:T(8,128)(2,1)S(1)}, bf16[2,1,24,384]{3,2,1,0:T(8,128)(2,1)S(1)}, u32[]{:S(2)}, u32[]{:S(2)}) collective-permute-start(bf16[2,1,24,384]{3,2,1,0:T(8,128)(2,1)S(1)} %get-tuple-element.130), channel_id=1, source_target_pairs={{0,1},{1,2},{2,3},{3,4},{4,5},{5,6},{6,7},{8,9},{9,10},{10,11},{11... | collective-permute-start | bytes 110600 | tf_op jit(solution)/shard_map/while/body/eval_jaxpr/ppermute | solution.py:13
  103.1 7.4 %fusion.58 = f32[2,8,24,1536]{3,2,1,0:T(8,128)} fusion(bf16[2,8,24,2304]{3,2,1,0:T(8,128)(2,1)S(1)} %slice_dynamic-update-slice_fusion.26, bf16[2304,1536,1,1]{1,0,3,2:T(8,128)(2,1)} %bitcast.35), kind=kOutput, calls=%fused_computation.67.clone.1 | convolution fusion | flops 2717908992 | bytes 11206656 | tf_op jit(solution)/shard_map/while/body/eval_jaxpr/dot_general | solution.py:28
  111.9 3.2 %collective-permute-done.3 = bf16[2,10,1,384]{3,2,1,0:T(2,128)(2,1)S(1)} collective-permute-done((bf16[2,10,1,384]{3,2,1,0:T(2,128)(2,1)S(1)}, bf16[2,10,1,384]{3,2,1,0:T(2,128)(2,1)S(1)}, u32[]{:S(2)}, u32[]{:S(2)}) %collective-permute-start.3) | collective-permute-done | bytes 15392 | tf_op jit(solution)/shard_map/while/body/eval_jaxpr/ppermute | solution.py:14
  115.9 7.3 %fusion.69 = f32[2,8,24,1536]{3,2,1,0:T(8,128)S(1)} fusion(f32[2,8,24,1536]{3,2,1,0:T(8,128)S(1)} %copy-done.6, bf16[2,8,24,3456]{3,2,1,0:T(8,128)(2,1)S(1)} %fusion.68, bf16[3456,1536,1,1]{1,0,3,2:T(8,128)(2,1)} %bitcast.34, f32[1536]{0:T(1024)S(1)} %get-tuple-element.162), kind=kOutput, calls=%fused_computation.1.clone.1 | convolution fusion | flops 4078043136 | bytes 17995776 | tf_op jit(solution)/shard_map/while/body/eval_jaxpr/dot_general | solution.py:28
  124.6 3.4 %collective-permute-start = (bf16[2,1,24,384]{3,2,1,0:T(8,128)(2,1)S(1)}, bf16[2,1,24,384]{3,2,1,0:T(8,128)(2,1)S(1)}, u32[]{:S(2)}, u32[]{:S(2)}) collective-permute-start(bf16[2,1,24,384]{3,2,1,0:T(8,128)(2,1)S(1)} %get-tuple-element.130), channel_id=1, source_target_pairs={{0,1},{1,2},{2,3},{3,4},{4,5},{5,6},{6,7},{8,9},{9,10},{10,11},{11... | collective-permute-start | bytes 110600 | tf_op jit(solution)/shard_map/while/body/eval_jaxpr/ppermute | solution.py:13
  135.0 7.4 %fusion.58 = f32[2,8,24,1536]{3,2,1,0:T(8,128)} fusion(bf16[2,8,24,2304]{3,2,1,0:T(8,128)(2,1)S(1)} %slice_dynamic-update-slice_fusion.26, bf16[2304,1536,1,1]{1,0,3,2:T(8,128)(2,1)} %bitcast.35), kind=kOutput, calls=%fused_computation.67.clone.1 | convolution fusion | flops 2717908992 | bytes 11206656 | tf_op jit(solution)/shard_map/while/body/eval_jaxpr/dot_general | solution.py:28
  143.8 3.2 %collective-permute-done.3 = bf16[2,10,1,384]{3,2,1,0:T(2,128)(2,1)S(1)} collective-permute-done((bf16[2,10,1,384]{3,2,1,0:T(2,128)(2,1)S(1)}, bf16[2,10,1,384]{3,2,1,0:T(2,128)(2,1)S(1)}, u32[]{:S(2)}, u32[]{:S(2)}) %collective-permute-start.3) | collective-permute-done | bytes 15392 | tf_op jit(solution)/shard_map/while/body/eval_jaxpr/ppermute | solution.py:14
  147.8 7.3 %fusion.69 = f32[2,8,24,1536]{3,2,1,0:T(8,128)S(1)} fusion(f32[2,8,24,1536]{3,2,1,0:T(8,128)S(1)} %copy-done.6, bf16[2,8,24,3456]{3,2,1,0:T(8,128)(2,1)S(1)} %fusion.68, bf16[3456,1536,1,1]{1,0,3,2:T(8,128)(2,1)} %bitcast.34, f32[1536]{0:T(1024)S(1)} %get-tuple-element.162), kind=kOutput, calls=%fused_computation.1.clone.1 | convolution fusion | flops 4078043136 | bytes 17995776 | tf_op jit(solution)/shard_map/while/body/eval_jaxpr/dot_general | solution.py:28
  (152 shorter events, 44.8 us)
Async XLA Ops:
  0.6 7.8 %copy-start.4 = (bf16[4,2,8,24,256]{4,3,2,1,0:T(8,128)(2,1)S(1)}, bf16[4,2,8,24,256]{4,3,2,1,0:T(8,128)(2,1)}, u32[]{:S(2)}) copy-start(bf16[4,2,8,24,256]{4,3,2,1,0:T(8,128)(2,1)} %param.8) | copy-start | bytes 2359300
  1.7 6.7 %collective-permute-start.4 = (bf16[4,2,1,24,256]{4,3,2,1,0:T(8,128)(2,1)S(1)}, bf16[4,2,1,24,256]{4,3,2,1,0:T(8,128)(2,1)S(1)}, u32[]{:S(2)}, u32[]{:S(2)}) collective-permute-start(bf16[4,2,1,24,256]{4,3,2,1,0:T(8,128)(2,1)S(1)} %get-tuple-element.73), channel_id=1, source_target_pairs={{0,1},{1,2},{2,3},{3,4},{4,5},{5,6},{6,7},{8,9},{9,10},{10,11},{11... | collective-permute-start | bytes 294920 | tf_op jit(solution)/shard_map/ppermute | solution.py:13
  6.3 18.7 %copy-start = (bf16[2,8,24,384]{3,2,1,0:T(8,128)(2,1)S(1)}, bf16[2,8,24,384]{3,2,1,0:T(8,128)(2,1)}, u32[]{:S(2)}) copy-start(bf16[2,8,24,384]{3,2,1,0:T(8,128)(2,1)} %param.12) | copy-start | bytes 884740
  6.3 18.7 %copy-start.2 = (f32[2,8,24,384]{3,2,1,0:T(8,128)S(1)}, f32[2,8,24,384]{3,2,1,0:T(8,128)}, u32[]{:S(2)}) copy-start(f32[2,8,24,384]{3,2,1,0:T(8,128)} %param.13) | copy-start | bytes 1769476
  6.3 18.7 %copy-start.5 = (f32[1536]{0:T(1024)S(1)}, f32[1536]{0:T(1024)}, u32[]{:S(2)}) copy-start(f32[1536]{0:T(1024)} %param.11) | copy-start | bytes 18436
  6.3 6.1 %collective-permute-start.5 = (bf16[4,2,1,24,256]{4,3,2,1,0:T(8,128)(2,1)S(1)}, bf16[4,2,1,24,256]{4,3,2,1,0:T(8,128)(2,1)S(1)}, u32[]{:S(2)}, u32[]{:S(2)}) collective-permute-start(bf16[4,2,1,24,256]{4,3,2,1,0:T(8,128)(2,1)S(1)} %get-tuple-element.72), channel_id=1, source_target_pairs={{1,0},{2,1},{3,2},{4,3},{5,4},{6,5},{7,6},{9,8},{10,9},{11,10},{12... | collective-permute-start | bytes 294920 | tf_op jit(solution)/shard_map/ppermute | solution.py:14
  13.5 5.2 %collective-permute-start.6 = (bf16[4,2,10,1,256]{4,3,2,1,0:T(2,128)(2,1)S(1)}, bf16[4,2,10,1,256]{4,3,2,1,0:T(2,128)(2,1)S(1)}, u32[]{:S(2)}, u32[]{:S(2)}) collective-permute-start(bf16[4,2,10,1,256]{4,3,2,1,0:T(2,128)(2,1)S(1)} %get-tuple-element.70), channel_id=1, source_target_pairs={{0,8},{8,16},{16,24},{1,9},{9,17},{17,25},{2,10},{10,18},{18,26},{... | collective-permute-start | bytes 122888 | tf_op jit(solution)/shard_map/ppermute | solution.py:13
  17.3 5.6 %collective-permute-start.7 = (bf16[4,2,10,1,256]{4,3,2,1,0:T(2,128)(2,1)S(1)}, bf16[4,2,10,1,256]{4,3,2,1,0:T(2,128)(2,1)S(1)}, u32[]{:S(2)}, u32[]{:S(2)}) collective-permute-start(bf16[4,2,10,1,256]{4,3,2,1,0:T(2,128)(2,1)S(1)} %get-tuple-element.71), channel_id=1, source_target_pairs={{8,0},{16,8},{24,16},{9,1},{17,9},{25,17},{10,2},{18,10},{26,18},{... | collective-permute-start | bytes 122888 | tf_op jit(solution)/shard_map/ppermute | solution.py:14
  25.0 5.6 %collective-permute-start = (bf16[2,1,24,384]{3,2,1,0:T(8,128)(2,1)S(1)}, bf16[2,1,24,384]{3,2,1,0:T(8,128)(2,1)S(1)}, u32[]{:S(2)}, u32[]{:S(2)}) collective-permute-start(bf16[2,1,24,384]{3,2,1,0:T(8,128)(2,1)S(1)} %get-tuple-element.130), channel_id=1, source_target_pairs={{0,1},{1,2},{2,3},{3,4},{4,5},{5,6},{6,7},{8,9},{9,10},{10,11},{11... | collective-permute-start | bytes 110600 | tf_op jit(solution)/shard_map/while/body/eval_jaxpr/ppermute | solution.py:13
  28.1 5.3 %collective-permute-start.1 = (bf16[2,1,24,384]{3,2,1,0:T(8,128)(2,1)S(1)}, bf16[2,1,24,384]{3,2,1,0:T(8,128)(2,1)S(1)}, u32[]{:S(2)}, u32[]{:S(2)}) collective-permute-start(bf16[2,1,24,384]{3,2,1,0:T(8,128)(2,1)S(1)} %get-tuple-element.131), channel_id=1, source_target_pairs={{1,0},{2,1},{3,2},{4,3},{5,4},{6,5},{7,6},{9,8},{10,9},{11,10},{12... | collective-permute-start | bytes 110600 | tf_op jit(solution)/shard_map/while/body/eval_jaxpr/ppermute | solution.py:14
  33.4 12.5 %collective-permute-start.2 = (bf16[2,10,1,384]{3,2,1,0:T(2,128)(2,1)S(1)}, bf16[2,10,1,384]{3,2,1,0:T(2,128)(2,1)S(1)}, u32[]{:S(2)}, u32[]{:S(2)}) collective-permute-start(bf16[2,10,1,384]{3,2,1,0:T(2,128)(2,1)S(1)} %get-tuple-element.132), channel_id=1, source_target_pairs={{0,8},{8,16},{16,24},{1,9},{9,17},{17,25},{2,10},{10,18},{18,26},{... | collective-permute-start | bytes 46088 | tf_op jit(solution)/shard_map/while/body/eval_jaxpr/ppermute | solution.py:13
  44.7 4.8 %collective-permute-start.3 = (bf16[2,10,1,384]{3,2,1,0:T(2,128)(2,1)S(1)}, bf16[2,10,1,384]{3,2,1,0:T(2,128)(2,1)S(1)}, u32[]{:S(2)}, u32[]{:S(2)}) collective-permute-start(bf16[2,10,1,384]{3,2,1,0:T(2,128)(2,1)S(1)} %get-tuple-element.133), channel_id=1, source_target_pairs={{8,0},{16,8},{24,16},{9,1},{17,9},{25,17},{10,2},{18,10},{26,18},{... | collective-permute-start | bytes 46088 | tf_op jit(solution)/shard_map/while/body/eval_jaxpr/ppermute | solution.py:14
  59.0 5.8 %collective-permute-start = (bf16[2,1,24,384]{3,2,1,0:T(8,128)(2,1)S(1)}, bf16[2,1,24,384]{3,2,1,0:T(8,128)(2,1)S(1)}, u32[]{:S(2)}, u32[]{:S(2)}) collective-permute-start(bf16[2,1,24,384]{3,2,1,0:T(8,128)(2,1)S(1)} %get-tuple-element.130), channel_id=1, source_target_pairs={{0,1},{1,2},{2,3},{3,4},{4,5},{5,6},{6,7},{8,9},{9,10},{10,11},{11... | collective-permute-start | bytes 110600 | tf_op jit(solution)/shard_map/while/body/eval_jaxpr/ppermute | solution.py:13
  62.2 5.3 %collective-permute-start.1 = (bf16[2,1,24,384]{3,2,1,0:T(8,128)(2,1)S(1)}, bf16[2,1,24,384]{3,2,1,0:T(8,128)(2,1)S(1)}, u32[]{:S(2)}, u32[]{:S(2)}) collective-permute-start(bf16[2,1,24,384]{3,2,1,0:T(8,128)(2,1)S(1)} %get-tuple-element.131), channel_id=1, source_target_pairs={{1,0},{2,1},{3,2},{4,3},{5,4},{6,5},{7,6},{9,8},{10,9},{11,10},{12... | collective-permute-start | bytes 110600 | tf_op jit(solution)/shard_map/while/body/eval_jaxpr/ppermute | solution.py:14
  67.6 12.2 %collective-permute-start.2 = (bf16[2,10,1,384]{3,2,1,0:T(2,128)(2,1)S(1)}, bf16[2,10,1,384]{3,2,1,0:T(2,128)(2,1)S(1)}, u32[]{:S(2)}, u32[]{:S(2)}) collective-permute-start(bf16[2,10,1,384]{3,2,1,0:T(2,128)(2,1)S(1)} %get-tuple-element.132), channel_id=1, source_target_pairs={{0,8},{8,16},{16,24},{1,9},{9,17},{17,25},{2,10},{10,18},{18,26},{... | collective-permute-start | bytes 46088 | tf_op jit(solution)/shard_map/while/body/eval_jaxpr/ppermute | solution.py:13
  78.5 4.7 %collective-permute-start.3 = (bf16[2,10,1,384]{3,2,1,0:T(2,128)(2,1)S(1)}, bf16[2,10,1,384]{3,2,1,0:T(2,128)(2,1)S(1)}, u32[]{:S(2)}, u32[]{:S(2)}) collective-permute-start(bf16[2,10,1,384]{3,2,1,0:T(2,128)(2,1)S(1)} %get-tuple-element.133), channel_id=1, source_target_pairs={{8,0},{16,8},{24,16},{9,1},{17,9},{25,17},{10,2},{18,10},{26,18},{... | collective-permute-start | bytes 46088 | tf_op jit(solution)/shard_map/while/body/eval_jaxpr/ppermute | solution.py:14
  92.6 5.9 %collective-permute-start = (bf16[2,1,24,384]{3,2,1,0:T(8,128)(2,1)S(1)}, bf16[2,1,24,384]{3,2,1,0:T(8,128)(2,1)S(1)}, u32[]{:S(2)}, u32[]{:S(2)}) collective-permute-start(bf16[2,1,24,384]{3,2,1,0:T(8,128)(2,1)S(1)} %get-tuple-element.130), channel_id=1, source_target_pairs={{0,1},{1,2},{2,3},{3,4},{4,5},{5,6},{6,7},{8,9},{9,10},{10,11},{11... | collective-permute-start | bytes 110600 | tf_op jit(solution)/shard_map/while/body/eval_jaxpr/ppermute | solution.py:13
  96.0 5.3 %collective-permute-start.1 = (bf16[2,1,24,384]{3,2,1,0:T(8,128)(2,1)S(1)}, bf16[2,1,24,384]{3,2,1,0:T(8,128)(2,1)S(1)}, u32[]{:S(2)}, u32[]{:S(2)}) collective-permute-start(bf16[2,1,24,384]{3,2,1,0:T(8,128)(2,1)S(1)} %get-tuple-element.131), channel_id=1, source_target_pairs={{1,0},{2,1},{3,2},{4,3},{5,4},{6,5},{7,6},{9,8},{10,9},{11,10},{12... | collective-permute-start | bytes 110600 | tf_op jit(solution)/shard_map/while/body/eval_jaxpr/ppermute | solution.py:14
  101.4 10.3 %collective-permute-start.2 = (bf16[2,10,1,384]{3,2,1,0:T(2,128)(2,1)S(1)}, bf16[2,10,1,384]{3,2,1,0:T(2,128)(2,1)S(1)}, u32[]{:S(2)}, u32[]{:S(2)}) collective-permute-start(bf16[2,10,1,384]{3,2,1,0:T(2,128)(2,1)S(1)} %get-tuple-element.132), channel_id=1, source_target_pairs={{0,8},{8,16},{16,24},{1,9},{9,17},{17,25},{2,10},{10,18},{18,26},{... | collective-permute-start | bytes 46088 | tf_op jit(solution)/shard_map/while/body/eval_jaxpr/ppermute | solution.py:13
  110.4 4.7 %collective-permute-start.3 = (bf16[2,10,1,384]{3,2,1,0:T(2,128)(2,1)S(1)}, bf16[2,10,1,384]{3,2,1,0:T(2,128)(2,1)S(1)}, u32[]{:S(2)}, u32[]{:S(2)}) collective-permute-start(bf16[2,10,1,384]{3,2,1,0:T(2,128)(2,1)S(1)} %get-tuple-element.133), channel_id=1, source_target_pairs={{8,0},{16,8},{24,16},{9,1},{17,9},{25,17},{10,2},{18,10},{26,18},{... | collective-permute-start | bytes 46088 | tf_op jit(solution)/shard_map/while/body/eval_jaxpr/ppermute | solution.py:14
  124.6 5.9 %collective-permute-start = (bf16[2,1,24,384]{3,2,1,0:T(8,128)(2,1)S(1)}, bf16[2,1,24,384]{3,2,1,0:T(8,128)(2,1)S(1)}, u32[]{:S(2)}, u32[]{:S(2)}) collective-permute-start(bf16[2,1,24,384]{3,2,1,0:T(8,128)(2,1)S(1)} %get-tuple-element.130), channel_id=1, source_target_pairs={{0,1},{1,2},{2,3},{3,4},{4,5},{5,6},{6,7},{8,9},{9,10},{10,11},{11... | collective-permute-start | bytes 110600 | tf_op jit(solution)/shard_map/while/body/eval_jaxpr/ppermute | solution.py:13
  127.9 5.3 %collective-permute-start.1 = (bf16[2,1,24,384]{3,2,1,0:T(8,128)(2,1)S(1)}, bf16[2,1,24,384]{3,2,1,0:T(8,128)(2,1)S(1)}, u32[]{:S(2)}, u32[]{:S(2)}) collective-permute-start(bf16[2,1,24,384]{3,2,1,0:T(8,128)(2,1)S(1)} %get-tuple-element.131), channel_id=1, source_target_pairs={{1,0},{2,1},{3,2},{4,3},{5,4},{6,5},{7,6},{9,8},{10,9},{11,10},{12... | collective-permute-start | bytes 110600 | tf_op jit(solution)/shard_map/while/body/eval_jaxpr/ppermute | solution.py:14
  133.3 10.3 %collective-permute-start.2 = (bf16[2,10,1,384]{3,2,1,0:T(2,128)(2,1)S(1)}, bf16[2,10,1,384]{3,2,1,0:T(2,128)(2,1)S(1)}, u32[]{:S(2)}, u32[]{:S(2)}) collective-permute-start(bf16[2,10,1,384]{3,2,1,0:T(2,128)(2,1)S(1)} %get-tuple-element.132), channel_id=1, source_target_pairs={{0,8},{8,16},{16,24},{1,9},{9,17},{17,25},{2,10},{10,18},{18,26},{... | collective-permute-start | bytes 46088 | tf_op jit(solution)/shard_map/while/body/eval_jaxpr/ppermute | solution.py:13
  142.3 4.7 %collective-permute-start.3 = (bf16[2,10,1,384]{3,2,1,0:T(2,128)(2,1)S(1)}, bf16[2,10,1,384]{3,2,1,0:T(2,128)(2,1)S(1)}, u32[]{:S(2)}, u32[]{:S(2)}) collective-permute-start(bf16[2,10,1,384]{3,2,1,0:T(2,128)(2,1)S(1)} %get-tuple-element.133), channel_id=1, source_target_pairs={{8,0},{16,8},{24,16},{9,1},{17,9},{25,17},{10,2},{18,10},{26,18},{... | collective-permute-start | bytes 46088 | tf_op jit(solution)/shard_map/while/body/eval_jaxpr/ppermute | solution.py:14
  (6 other events, 17.9 us)
where the time goes:
time: 158 us; the launch traced here: 157 us
  matrix products  58.5 us (37%)
  starting transfers between devices  48.5 us (31%)
  waiting for transfers between devices  31.7 us (20%)
  other arithmetic  11 us (7%)
  local copies, waits for them, and re-layouts  5.95 us (4%)
    dot_general x8, matrix products, conv_taps(): jnp.dot(flat_patches, flat_weights, preferred_element_type=jnp.float32)  58.5 us
    ppermute x10, starting transfers between devices, edge_swap(): from_prev = lax.ppermute(high_edge, axis_label, down_pairs)  32.1 us
    ppermute x10, waiting for transfers between devices, edge_swap(): from_next = lax.ppermute(low_edge, axis_label, up_pairs)  31.5 us
    ppermute x10, starting transfers between devices, edge_swap(): from_next = lax.ppermute(low_edge, axis_label, up_pairs)  16.4 us
    dynamic_update_slice x4, other arithmetic, local_run(): final_pair, all_hidden = lax.scan(step_fn, (h_init, c_init), frames_ext)  5.43 us
  transfers between devices with their start and end apart: 20, of which 11 were waited for; matrix products, arithmetic and copies ran while one was open for 21% of the time, Pallas kernels for 0%

commit v1 on v0

v1 whole, which is shorter than its diff:
```python
import jax
import jax.numpy as jnp
from jax import lax
from jax.experimental import pallas as pl
from jax.experimental.pallas import tpu as pltpu
from jax.sharding import PartitionSpec as P

MESH = pl.DeviceIdType.MESH
LANES = 128
SLOTS = ((-1, 0), (1, 0), (0, -1), (0, 1), (-1, -1), (-1, 1), (1, -1), (1, 1))


def sigmoid(x):
    return 0.5 * jnp.tanh(0.5 * x) + 0.5


def make_kernel(dims, row_count, col_count):
    T, SEQ, H, W, CX, CH = dims
    PR = SEQ * W
    M = H * PR
    NJ = CH // LANES

    def kernel(frames, wx_hbm, wh_hbm, bias_hbm, h_init, c_init, h_out, c_out,
               wx, wh, bias, rawx, rawh, cst, sx, sh, g, hf, ho, ecx, ech, acx, ach,
               wsem, rsem, osem, xsend, xrecv, hsend, hrecv):
        b = lax.axis_index("batch")
        row = lax.axis_index("rows")
        col = lax.axis_index("cols")

        def exists(dr, dc):
            r, c = row + dr, col + dc
            return (r >= 0) & (r < row_count) & (c >= 0) & (c < col_count)

        barrier = pltpu.get_barrier_semaphore()
        for dr, dc in SLOTS:
            @pl.when(exists(dr, dc))
            def _():
                pl.semaphore_signal(barrier, inc=1, device_id=(b, col + dc, row + dr), device_id_type=MESH)

        xloads = [[pltpu.make_async_copy(frames.at[t, s], rawx.at[t, :, s], rsem.at[t, s]) for s in range(SEQ)]
                  for t in range(T)]
        hloads = [pltpu.make_async_copy(h_init.at[s], rawh.at[:, s], rsem.at[T, s]) for s in range(SEQ)]
        cloads = [pltpu.make_async_copy(c_init.at[s], cst.at[:, s], rsem.at[T + 1, s]) for s in range(SEQ)]
        bload = pltpu.make_async_copy(bias_hbm, bias, wsem.at[2])
        wxload = pltpu.make_async_copy(wx_hbm, wx, wsem.at[0])
        whload = pltpu.make_async_copy(wh_hbm, wh, wsem.at[1])
        for t in range(T):
            for cp in xloads[t]:
                cp.start()
        for cp in hloads:
            cp.start()
        bload.start()
        wxload.start()
        for cp in cloads:
            cp.start()
        whload.start()

        def zero(cond, refs):
            @pl.when(cond)
            def _():
                for ref in refs:
                    ref[...] = jnp.zeros(ref.shape, ref.dtype)
        zero(row == 0, [sx.at[:, 1, 0:PR], sh.at[:, 1, 0:PR], acx.at[:, :, 0], ach.at[:, :, 0]])
        zero(row == row_count - 1, [sx.at[:, 1, M + PR:M + 2 * PR], sh.at[:, 1, M + PR:M + 2 * PR],
                                    acx.at[:, :, H + 1], ach.at[:, :, H + 1]])
        zero(col == 0, [acx.at[:, 0], ach.at[:, 0]])
        zero(col == col_count - 1, [acx.at[:, 1], ach.at[:, 1]])

        def copies(s_t, ec_t, ac_t, send, recv):
            s0 = s_t.at[1]
            parts = ((s0.at[pl.ds(M, PR)], s0.at[pl.ds(0, PR)]),
                     (s0.at[pl.ds(PR, PR)], s0.at[pl.ds(M + PR, PR)]),
                     (ec_t.at[1], ac_t.at[0, pl.ds(1, H)]),
                     (ec_t.at[0], ac_t.at[1, pl.ds(1, H)]),
                     (ec_t.at[1, H - 1], ac_t.at[0, 0]),
                     (ec_t.at[0, H - 1], ac_t.at[1, 0]),
                     (ec_t.at[1, 0], ac_t.at[0, H + 1]),
                     (ec_t.at[0, 0], ac_t.at[1, H + 1]))
            out = []
            for i, (dr, dc) in enumerate(SLOTS):
                cp = pltpu.make_async_remote_copy(
                    src_ref=parts[i][0], dst_ref=parts[i][1], send_sem=send.at[i], recv_sem=recv.at[i],
                    device_id=(b, col - dc, row - dr), device_id_type=MESH)
                out.append((exists(-dr, -dc), exists(dr, dc), cp))
            return out

        def start_all(cps):
            for can_send, _, cp in cps:
                @pl.when(can_send)
                def _():
                    cp.start()

        def wait_recv_all(cps):
            for _, can_recv, cp in cps:
                @pl.when(can_recv)
                def _():
                    cp.wait_recv()

        def wait_send_all(cps):
            for can_send, _, cp in cps:
                @pl.when(can_send)
                def _():
                    cp.wait_send()

        def xcopies(t):
            return copies(sx.at[t], ecx.at[t], acx.at[t], xsend.at[t], xrecv.at[t])

        def hcopies(t):
            return copies(sh.at[t], ech.at[t], ach.at[t], hsend.at[t], hrecv.at[t])

        def shifted(v):
            n = v.shape[0]
            c_idx = lax.broadcasted_iota(jnp.int32, v.shape, 0) % W
            left = jnp.where(c_idx == 0, 0.0, pltpu.roll(v, 1, 0))
            right = jnp.where(c_idx == W - 1, 0.0, pltpu.roll(v, n - 1, 0))
            return left, right

        def put_tile(s_ref, ec_ref, v, lane):
            left, right = shifted(v)
            s_ref[0, pl.ds(PR, M), pl.ds(lane, LANES)] = left.astype(jnp.bfloat16)
            s_ref[1, pl.ds(PR, M), pl.ds(lane, LANES)] = v.astype(jnp.bfloat16)
            s_ref[2, pl.ds(PR, M), pl.ds(lane, LANES)] = right.astype(jnp.bfloat16)
            j = lane // LANES
            hf[j] = v
            first = hf[j, pl.ds(0, H * SEQ, stride=W), :]
            last = hf[j, pl.ds(W - 1, H * SEQ, stride=W), :]
            ec_ref[0, :, :, pl.ds(lane, LANES)] = first.astype(jnp.bfloat16).reshape(H, SEQ, LANES)
            ec_ref[1, :, :, pl.ds(lane, LANES)] = last.astype(jnp.bfloat16).reshape(H, SEQ, LANES)

        def patch(s_ref, ac_ref, channels):
            i16 = lax.broadcasted_iota(jnp.int32, (16, channels), 0)
            for r in range(H):
                for side in range(2):
                    for s in range(SEQ):
                        pos = s * W if side == 0 else s * W + W - 1
                        base = PR * (r + 1) + pos // 16 * 16
                        dxi = 2 * side
                        old = s_ref[dxi, pl.ds(base, 16), :].astype(jnp.float32)
                        halo = ac_ref[side, r + 1, s:s + 1, :].astype(jnp.float32)
                        s_ref[dxi, pl.ds(base, 16), :] = jnp.where(i16 == pos % 16, halo, old).astype(jnp.bfloat16)
            pos_idx = lax.broadcasted_iota(jnp.int32, (PR, channels), 0)
            for r in (0, H + 1):
                v = s_ref[1, pl.ds(PR * r, PR), :].astype(jnp.float32)
                for side in range(2):
                    out = pltpu.roll(v, 1 if side == 0 else PR - 1, 0)
                    for s in range(SEQ):
                        halo = ac_ref[side, r, s:s + 1, :].astype(jnp.float32)
                        out = jnp.where(pos_idx == (s * W if side == 0 else s * W + W - 1), halo, out)
                    s_ref[2 * side, pl.ds(PR * r, PR), :] = out.astype(jnp.bfloat16)

        def conv(s_ref, w_ref, j):
            lhs = jnp.concatenate([s_ref[dx, pl.ds(dy * PR, M), :] for dy in range(3) for dx in range(3)], axis=1)
            rhs = jnp.concatenate([w_ref[:, pl.ds(q * CH + j * LANES, LANES)] for q in range(4)], axis=1)
            return jnp.dot(lhs, rhs, preferred_element_type=jnp.float32)

        def x_phase(t):
            for j in range(NJ):
                bj = jnp.concatenate([bias[:, pl.ds(q * CH + j * LANES, LANES)] for q in range(4)], axis=1)
                g[j] = conv(sx.at[t], wx, j) + bj

        def out_copies(t):
            return [pltpu.make_async_copy(ho.at[t, s], h_out.at[t, s], osem.at[t, s]) for s in range(SEQ)]

        def h_phase(t, last):
            for j in range(NJ):
                lane = j * LANES
                gates = conv(sh.at[t], wh, j) + g[j]
                gi = sigmoid(gates[:, 0:LANES])
                gf = sigmoid(gates[:, LANES:2 * LANES])
                go = sigmoid(gates[:, 2 * LANES:3 * LANES])
                gg = jnp.tanh(gates[:, 3 * LANES:])
                c_old = cst[:, :, :, pl.ds(lane, LANES)].reshape(M, LANES)
                c_new = gf * c_old + gi * gg
                cst[:, :, :, pl.ds(lane, LANES)] = c_new.reshape(H, SEQ, W, LANES)
                h_new = go * jnp.tanh(c_new)
                h4 = h_new.reshape(H, SEQ, W, LANES)
                for s in range(SEQ):
                    ho[t, s, :, :, pl.ds(lane, LANES)] = h4[:, s].astype(jnp.bfloat16)
                if not last:
                    put_tile(sh.at[t + 1], ech.at[t + 1], h_new, lane)

        def fill(raw, s_ref, ec_ref, channels):
            for k in range(channels // LANES):
                lane = k * LANES
                v = raw[:, :, :, pl.ds(lane, LANES)].astype(jnp.float32).reshape(M, LANES)
                put_tile(s_ref, ec_ref, v, lane)

        for cp in xloads[0]:
            cp.wait()
        fill(rawx.at[0], sx.at[0], ecx.at[0], CX)
        for cp in hloads:
            cp.wait()
        fill(rawh, sh.at[0], ech.at[0], CH)
        n_near = sum(exists(dr, dc).astype(jnp.int32) for dr, dc in SLOTS)
        pl.semaphore_wait(barrier, n_near)
        start_all(xcopies(0))
        start_all(hcopies(0))
        for t in range(1, T):
            for cp in xloads[t]:
                cp.wait()

        @pl.loop(1, T)
        def _(t):
            fill(rawx.at[t], sx.at[t], ecx.at[t], CX)
            start_all(xcopies(t))

        bload.wait()
        for cp in cloads:
            cp.wait()
        wait_recv_all(xcopies(0))
        patch(sx.at[0], acx.at[0], CX)
        wxload.wait()
        x_phase(0)
        whload.wait()

        @pl.loop(0, T - 1)
        def _(t):
            wait_recv_all(hcopies(t))
            patch(sh.at[t], ach.at[t], CH)
            h_phase(t, False)
            for cp in out_copies(t):
                cp.start()
            start_all(hcopies(t + 1))
            wait_recv_all(xcopies(t + 1))
            patch(sx.at[t + 1], acx.at[t + 1], CX)
            x_phase(t + 1)

        wait_recv_all(hcopies(T - 1))
        patch(sh.at[T - 1], ach.at[T - 1], CH)
        h_phase(T - 1, True)
        for cp in out_copies(T - 1):
            cp.start()
        c_copies = [pltpu.make_async_copy(cst.at[:, s], c_out.at[s], osem.at[T, s]) for s in range(SEQ)]
        for cp in c_copies:
            cp.start()
        for t in range(T):
            wait_send_all(xcopies(t))
            wait_send_all(hcopies(t))
            for cp in out_copies(t):
                cp.wait()
        for cp in c_copies:
            cp.wait()

    return kernel


def solution(mesh):
    row_count = mesh.shape["rows"]
    col_count = mesh.shape["cols"]
    frame_spec = P(None, "batch", "rows", "cols", None)
    state_spec = P("batch", "rows", "cols", None)

    def local_run(frames, w_x, w_h, gate_bias, h_init, c_init):
        T, SEQ, H, W, CX = frames.shape
        CH = h_init.shape[-1]
        NG = 4 * CH
        PR = SEQ * W
        M = H * PR
        bf, f32 = jnp.bfloat16, jnp.float32
        hbm = pl.BlockSpec(memory_space=pl.ANY)
        kernel = make_kernel((T, SEQ, H, W, CX, CH), row_count, col_count)
        return pl.pallas_call(
            kernel,
            out_shape=(jax.ShapeDtypeStruct((T, SEQ, H, W, CH), bf), jax.ShapeDtypeStruct((SEQ, H, W, CH), f32)),
            in_specs=[hbm] * 6,
            out_specs=(hbm, hbm),
            scratch_shapes=[
                pltpu.VMEM((9 * CX, NG), bf), pltpu.VMEM((9 * CH, NG), bf), pltpu.VMEM((1, NG), f32),
                pltpu.VMEM((T, H, SEQ, W, CX), bf), pltpu.VMEM((H, SEQ, W, CH), bf), pltpu.VMEM((H, SEQ, W, CH), f32),
                pltpu.VMEM((T, 3, M + 2 * PR, CX), bf), pltpu.VMEM((T, 3, M + 2 * PR, CH), bf),
                pltpu.VMEM((CH // LANES, M, 4 * LANES), f32), pltpu.VMEM((max(CH, CX) // LANES, M, LANES), f32),
                pltpu.VMEM((T, SEQ, H, W, CH), bf),
                pltpu.VMEM((T, 2, H, SEQ, CX), bf), pltpu.VMEM((T, 2, H, SEQ, CH), bf),
                pltpu.VMEM((T, 2, H + 2, SEQ, CX), bf), pltpu.VMEM((T, 2, H + 2, SEQ, CH), bf),
                pltpu.SemaphoreType.DMA((3,)), pltpu.SemaphoreType.DMA((T + 2, SEQ)),
                pltpu.SemaphoreType.DMA((T + 1, SEQ)),
                pltpu.SemaphoreType.DMA((T, 8)), pltpu.SemaphoreType.DMA((T, 8)),
                pltpu.SemaphoreType.DMA((T, 8)), pltpu.SemaphoreType.DMA((T, 8)),
            ],
            compiler_params=pltpu.CompilerParams(
                collective_id=0, has_side_effects=True, vmem_limit_bytes=60 * 1024 * 1024),
        )(frames, w_x.reshape(9 * CX, NG), w_h.reshape(9 * CH, NG), gate_bias.reshape(1, NG), h_init, c_init)

    return jax.shard_map(local_run, mesh=mesh,
                         in_specs=(frame_spec, P(), P(), P(), state_spec, state_spec),
                         out_specs=(frame_spec, state_spec), check_vma=False)
```

time: 158 us -> 49.3 us (0.31)
  matrix products: 58.5 us -> 0 us
  starting transfers between devices: 48.5 us -> 0 us
  Pallas kernels: 0 us -> 42.8 us
  waiting for transfers between devices: 31.7 us -> 0 us
  other arithmetic: 11 us -> 0 us
    dot_general x8 -> x0, matrix products: 58.5 us -> none  [conv_taps(): jnp.dot(flat_patches, flat_weights, preferred_element_type=jnp.float32)]
    ppermute x20 -> x0, starting transfers between devices: 48.5 us -> none  [the longest x10 32.1 us: edge_swap(): from_prev = lax.ppermute(high_edge, axis_label, down_pairs)]
    pallas_call x0 -> x1, Pallas kernels: none -> 42.8 us  [local_run(): pl.pallas_call(kernel, out_shape=(jax.ShapeDtypeStruct((T, SEQ, H, W, CH)...]
    ppermute x20 -> x0, waiting for transfers between devices: 31.7 us -> none  [the longest x10 31.5 us: edge_swap(): from_next = lax.ppermute(low_edge, axis_label, up_pairs)]
    dynamic_update_slice x4 -> x0, other arithmetic: 5.43 us -> none  [local_run(): final_pair, all_hidden = lax.scan(step_fn, (h_init, c_init), frames_ext)]
    while x28 -> x0, other arithmetic: 2.95 us -> none
    concatenate x5 -> x0, other arithmetic: 2.66 us -> none  [the longest x1 2.06 us: edge_swap(): return jnp.concatenate([from_prev, tile_arr, from_next], axis=split_dim)]
    unnamed x14 -> x2, local copies, waits for them, and re-layouts: 1.85 us -> 4.32 us
  transfers between devices with their start and end apart: 20 -> 0, of which waited for: 11 -> 0; matrix products, arithmetic and copies ran while one was open for 21% -> 0% of each run, Pallas kernels for 0% -> 0%
where the time goes in v1:
time: 49.3 us; the launch traced here: 49.1 us
  Pallas kernels  42.8 us (87%)
  local copies, waits for them, and re-layouts  5.61 us (11%)
  between operations  0.64 us (1%)
    pallas_call x1, Pallas kernels, local_run(): pl.pallas_call(kernel, out_shape=(jax.ShapeDtypeStruct((T, SEQ, H, W, CH)...  42.8 us
    unnamed x2, local copies, waits for them, and re-layouts  4.32 us
    reshape x1, local copies, waits for them, and re-layouts, local_run(): gate_bias.reshape(1, NG)  1.3 us

profile of v1, /device:TPU:97, one launch (start us, length us, event | category | flops | bytes accessed | tf_op | source)
XLA Modules:
  0.0 49.1 jit_solution(3044375361752146417)
XLA Ops:
  0.6 1.3 %reshape.15.bias_hbm = f32[1,1536]{1,0:T(1,128)} reshape(f32[1536]{0:T(1024)} %param.9) | data formatting | bytes 12288 | tf_op jit(solution)/shard_map/reshape | solution.py:282
  1.9 42.8 %shard_map.77 = (bf16[4,2,8,24,384]{4,3,2,1,0:T(8,128)(2,1)}, f32[2,8,24,384]{3,2,1,0:T(8,128)}) custom-call(bf16[4,2,8,24,256]{4,3,2,1,0:T(8,128)(2,1)} %frames.1, bf16[2304,1536]{1,0:T(8,128)(2,1)} %bitcast.3, bf16[3456,1536]{1,0:T(8,128)(2,1)} %bitcast.2, f32[1,1536]{1,0:T(1,128)} %reshape.15.bias_hbm, bf16[2,8,24,384]{3,2,1,0:T(8,128)(2,1)} %h_init.1, ...), custom_call_target="tpu_custom_call" | custom-call | tf_op jit(solution)/shard_map/pallas_call | solution.py:262
  44.7 2.4 %copy.10 = bf16[4,2,8,24,384]{4,3,2,1,0:T(8,128)(2,1)} copy(bf16[4,2,8,24,384]{4,3,2,1,0:T(8,128)(2,1)} %get-tuple-element.4) | data formatting | bytes 2359296
  47.1 1.9 %copy.11 = f32[2,8,24,384]{3,2,1,0:T(8,128)} copy(f32[2,8,24,384]{3,2,1,0:T(8,128)} %get-tuple-element.5) | data formatting | bytes 1179648

commit v2 on v1

--- a/solution.py
+++ b/solution.py
@@ -20,9 +20,9 @@
     M = H * PR
     NJ = CH // LANES
 
-    def kernel(frames, wx_hbm, wh_hbm, bias_hbm, h_init, c_init, h_out, c_out,
-               wx, wh, bias, rawx, rawh, cst, sx, sh, g, hf, ho, ecx, ech, acx, ach,
-               wsem, rsem, osem, xsend, xrecv, hsend, hrecv):
+    def kernel(frames, wx_hbm, wh_hbm, bias_hbm, h_init, c_init, ho, cst,
+               wx, wh, bias, rawx, rawh, sx, sh, g, hf, ecx, ech, acx, ach,
+               wsem, rsem, xsend, xrecv, hsend, hrecv):
         b = lax.axis_index("batch")
         row = lax.axis_index("rows")
         col = lax.axis_index("cols")
@@ -155,11 +155,8 @@
 
         def x_phase(t):
             for j in range(NJ):
-                bj = jnp.concatenate([bias[:, pl.ds(q * CH + j * LANES, LANES)] for q in range(4)], axis=1)
+                bj = jnp.concatenate([bias[pl.ds(q * CH + j * LANES, LANES)].reshape(1, LANES) for q in range(4)], axis=1)
                 g[j] = conv(sx.at[t], wx, j) + bj
-
-        def out_copies(t):
-            return [pltpu.make_async_copy(ho.at[t, s], h_out.at[t, s], osem.at[t, s]) for s in range(SEQ)]
 
         def h_phase(t, last):
             for j in range(NJ):
@@ -218,8 +215,6 @@
             wait_recv_all(hcopies(t))
             patch(sh.at[t], ach.at[t], CH)
             h_phase(t, False)
-            for cp in out_copies(t):
-                cp.start()
             start_all(hcopies(t + 1))
             wait_recv_all(xcopies(t + 1))
             patch(sx.at[t + 1], acx.at[t + 1], CX)
@@ -228,18 +223,9 @@
         wait_recv_all(hcopies(T - 1))
         patch(sh.at[T - 1], ach.at[T - 1], CH)
         h_phase(T - 1, True)
-        for cp in out_copies(T - 1):
-            cp.start()
-        c_copies = [pltpu.make_async_copy(cst.at[:, s], c_out.at[s], osem.at[T, s]) for s in range(SEQ)]
-        for cp in c_copies:
-            cp.start()
         for t in range(T):
             wait_send_all(xcopies(t))
             wait_send_all(hcopies(t))
-            for cp in out_copies(t):
-                cp.wait()
-        for cp in c_copies:
-            cp.wait()
 
     return kernel
 
@@ -258,28 +244,44 @@
         M = H * PR
         bf, f32 = jnp.bfloat16, jnp.float32
         hbm = pl.BlockSpec(memory_space=pl.ANY)
+        vmem = pl.BlockSpec(memory_space=pltpu.VMEM)
         kernel = make_kernel((T, SEQ, H, W, CX, CH), row_count, col_count)
-        return pl.pallas_call(
+        h_vmem, c_vmem = pl.pallas_call(
             kernel,
-            out_shape=(jax.ShapeDtypeStruct((T, SEQ, H, W, CH), bf), jax.ShapeDtypeStruct((SEQ, H, W, CH), f32)),
+            out_shape=(pltpu.VMEM((T, SEQ, H, W, CH), bf), pltpu.VMEM((H, SEQ, W, CH), f32)),
             in_specs=[hbm] * 6,
-            out_specs=(hbm, hbm),
+            out_specs=(vmem, vmem),
             scratch_shapes=[
-                pltpu.VMEM((9 * CX, NG), bf), pltpu.VMEM((9 * CH, NG), bf), pltpu.VMEM((1, NG), f32),
-                pltpu.VMEM((T, H, SEQ, W, CX), bf), pltpu.VMEM((H, SEQ, W, CH), bf), pltpu.VMEM((H, SEQ, W, CH), f32),
+                pltpu.VMEM((9 * CX, NG), bf), pltpu.VMEM((9 * CH, NG), bf), pltpu.VMEM((NG,), f32),
+                pltpu.VMEM((T, H, SEQ, W, CX), bf), pltpu.VMEM((H, SEQ, W, CH), bf),
                 pltpu.VMEM((T, 3, M + 2 * PR, CX), bf), pltpu.VMEM((T, 3, M + 2 * PR, CH), bf),
                 pltpu.VMEM((CH // LANES, M, 4 * LANES), f32), pltpu.VMEM((max(CH, CX) // LANES, M, LANES), f32),
-                pltpu.VMEM((T, SEQ, H, W, CH), bf),
                 pltpu.VMEM((T, 2, H, SEQ, CX), bf), pltpu.VMEM((T, 2, H, SEQ, CH), bf),
                 pltpu.VMEM((T, 2, H + 2, SEQ, CX), bf), pltpu.VMEM((T, 2, H + 2, SEQ, CH), bf),
                 pltpu.SemaphoreType.DMA((3,)), pltpu.SemaphoreType.DMA((T + 2, SEQ)),
-                pltpu.SemaphoreType.DMA((T + 1, SEQ)),
                 pltpu.SemaphoreType.DMA((T, 8)), pltpu.SemaphoreType.DMA((T, 8)),
                 pltpu.SemaphoreType.DMA((T, 8)), pltpu.SemaphoreType.DMA((T, 8)),
             ],
             compiler_params=pltpu.CompilerParams(
-                collective_id=0, has_side_effects=True, vmem_limit_bytes=60 * 1024 * 1024),
-        )(frames, w_x.reshape(9 * CX, NG), w_h.reshape(9 * CH, NG), gate_bias.reshape(1, NG), h_init, c_init)
+                collective_id=0, has_side_effects=True, vmem_limit_bytes=56 * 1024 * 1024),
+        )(frames, w_x.reshape(9 * CX, NG), w_h.reshape(9 * CH, NG), gate_bias, h_init, c_init)
+
+        def write_out(h_ref, c_ref, h_out, c_out, sem):
+            cps = [pltpu.make_async_copy(h_ref, h_out, sem.at[SEQ])]
+            cps += [pltpu.make_async_copy(c_ref.at[:, s], c_out.at[s], sem.at[s]) for s in range(SEQ)]
+            for cp in cps:
+                cp.start()
+            for cp in cps:
+                cp.wait()
+
+        return pl.pallas_call(
+            write_out,
+            out_shape=(jax.ShapeDtypeStruct((T, SEQ, H, W, CH), bf), jax.ShapeDtypeStruct((SEQ, H, W, CH), f32)),
+            in_specs=[vmem] * 2,
+            out_specs=(hbm, hbm),
+            scratch_shapes=[pltpu.SemaphoreType.DMA((SEQ + 1,))],
+            compiler_params=pltpu.CompilerParams(vmem_limit_bytes=1024 * 1024),
+        )(h_vmem, c_vmem)
 
     return jax.shard_map(local_run, mesh=mesh,
                          in_specs=(frame_spec, P(), P(), P(), state_spec, state_spec),

time: 49.3 us -> 43.9 us (0.89)
  local copies, waits for them, and re-layouts: 5.61 us -> 0 us
    unnamed x2 -> x0, local copies, waits for them, and re-layouts: 4.32 us -> none
    reshape x1 -> x0, local copies, waits for them, and re-layouts: 1.3 us -> none  [local_run(): gate_bias.reshape(1, NG)]
    pallas_call x1 -> x2, Pallas kernels: 42.8 us -> 43.2 us  [the longest x1 42 us: local_run(): pl.pallas_call(kernel, out_shape=(pltpu.VMEM((T, SEQ, H, W, CH), bf), plt...]
where the time goes in v2:
time: 43.9 us; the launch traced here: 43.8 us
  Pallas kernels  43.2 us (98%)
  between operations  0.64 us (1%)
    pallas_call x1, Pallas kernels, local_run(): pl.pallas_call(kernel, out_shape=(pltpu.VMEM((T, SEQ, H, W, CH), bf), plt...  42 us
    pallas_call x1, Pallas kernels, local_run(): pl.pallas_call(write_out, out_shape=(jax.ShapeDtypeStruct((T, SEQ, H, W,...  1.23 us

profile of v2, /device:TPU:97, one launch (start us, length us, event | category | flops | bytes accessed | tf_op | source)
XLA Modules:
  0.0 43.8 jit_solution(14021722373055457298)
XLA Ops:
  0.6 42.0 %shard_map.77 = (bf16[4,2,8,24,384]{4,3,2,1,0:T(8,128)(2,1)S(1)}, f32[8,2,24,384]{3,2,1,0:T(8,128)S(1)}) custom-call(bf16[4,2,8,24,256]{4,3,2,1,0:T(8,128)(2,1)} %frames.1, bf16[2304,1536]{1,0:T(8,128)(2,1)} %bitcast.3, bf16[3456,1536]{1,0:T(8,128)(2,1)} %bitcast.2, f32[1536]{0:T(1024)} %bias_hbm.1, bf16[2,8,24,384]{3,2,1,0:T(8,128)(2,1)} %h_init.1, ...), custom_call_target="tpu_custom_call" | custom-call | tf_op jit(solution)/shard_map/pallas_call | solution.py:249
  42.6 1.2 %shard_map.78 = (bf16[4,2,8,24,384]{4,3,2,1,0:T(8,128)(2,1)}, f32[2,8,24,384]{3,2,1,0:T(8,128)}) custom-call(bf16[4,2,8,24,384]{4,3,2,1,0:T(8,128)(2,1)S(1)} %get-tuple-element.4.h_ref, f32[8,2,24,384]{3,2,1,0:T(8,128)S(1)} %get-tuple-element.5.c_ref), custom_call_target="tpu_custom_call" | custom-call | tf_op jit(solution)/shard_map/pallas_call | solution.py:277

commit v3 on v2

--- a/solution.py
+++ b/solution.py
@@ -41,19 +41,16 @@
                   for t in range(T)]
         hloads = [pltpu.make_async_copy(h_init.at[s], rawh.at[:, s], rsem.at[T, s]) for s in range(SEQ)]
         cloads = [pltpu.make_async_copy(c_init.at[s], cst.at[:, s], rsem.at[T + 1, s]) for s in range(SEQ)]
-        bload = pltpu.make_async_copy(bias_hbm, bias, wsem.at[2])
-        wxload = pltpu.make_async_copy(wx_hbm, wx, wsem.at[0])
-        whload = pltpu.make_async_copy(wh_hbm, wh, wsem.at[1])
-        for t in range(T):
-            for cp in xloads[t]:
-                cp.start()
-        for cp in hloads:
+        bload = pltpu.make_async_copy(bias_hbm, bias, wsem.at[0])
+
+        def wloads(w_hbm, w_vmem, channels, first_sem):
+            parts = (pl.ds(4 * channels, channels), pl.ds(0, 4 * channels), pl.ds(5 * channels, 4 * channels))
+            return [pltpu.make_async_copy(w_hbm.at[p], w_vmem.at[p], wsem.at[first_sem + i]) for i, p in enumerate(parts)]
+        wxloads = wloads(wx_hbm, wx, CX, 1)
+        whloads = wloads(wh_hbm, wh, CH, 4)
+        later = [cp for t in range(1, T) for cp in xloads[t]]
+        for cp in [*xloads[0], *hloads, bload, wxloads[0], whloads[0], *later, *wxloads[1:], *cloads, *whloads[1:]]:
             cp.start()
-        bload.start()
-        wxload.start()
-        for cp in cloads:
-            cp.start()
-        whload.start()
 
         def zero(cond, refs):
             @pl.when(cond)
@@ -109,23 +106,21 @@
             return copies(sh.at[t], ech.at[t], ach.at[t], hsend.at[t], hrecv.at[t])
 
         def shifted(v):
-            n = v.shape[0]
-            c_idx = lax.broadcasted_iota(jnp.int32, v.shape, 0) % W
-            left = jnp.where(c_idx == 0, 0.0, pltpu.roll(v, 1, 0))
-            right = jnp.where(c_idx == W - 1, 0.0, pltpu.roll(v, n - 1, 0))
-            return left, right
-
-        def put_tile(s_ref, ec_ref, v, lane):
+            n, channels = v.shape
+            c_idx = lax.broadcasted_iota(jnp.int32, (1, W, channels), 1)
+            left = jnp.where(c_idx == 0, 0.0, pltpu.roll(v, 1, 0).reshape(n // W, W, channels))
+            right = jnp.where(c_idx == W - 1, 0.0, pltpu.roll(v, n - 1, 0).reshape(n // W, W, channels))
+            return left.reshape(n, channels), right.reshape(n, channels)
+
+        def put_rows(s_ref, v, first, lanes):
             left, right = shifted(v)
-            s_ref[0, pl.ds(PR, M), pl.ds(lane, LANES)] = left.astype(jnp.bfloat16)
-            s_ref[1, pl.ds(PR, M), pl.ds(lane, LANES)] = v.astype(jnp.bfloat16)
-            s_ref[2, pl.ds(PR, M), pl.ds(lane, LANES)] = right.astype(jnp.bfloat16)
-            j = lane // LANES
-            hf[j] = v
-            first = hf[j, pl.ds(0, H * SEQ, stride=W), :]
-            last = hf[j, pl.ds(W - 1, H * SEQ, stride=W), :]
-            ec_ref[0, :, :, pl.ds(lane, LANES)] = first.astype(jnp.bfloat16).reshape(H, SEQ, LANES)
-            ec_ref[1, :, :, pl.ds(lane, LANES)] = last.astype(jnp.bfloat16).reshape(H, SEQ, LANES)
+            for dx, form in enumerate((left, v, right)):
+                s_ref[dx, pl.ds(first, v.shape[0]), lanes] = form.astype(jnp.bfloat16)
+
+        def put_edges(ec_ref, j):
+            for side in range(2):
+                edge = hf[j, pl.ds(side * (W - 1), H * SEQ, stride=W), :]
+                ec_ref[side, :, :, pl.ds(j * LANES, LANES)] = edge.astype(jnp.bfloat16).reshape(H, SEQ, LANES)
 
         def patch(s_ref, ac_ref, channels):
             i16 = lax.broadcasted_iota(jnp.int32, (16, channels), 0)
@@ -148,20 +143,25 @@
                         out = jnp.where(pos_idx == (s * W if side == 0 else s * W + W - 1), halo, out)
                     s_ref[2 * side, pl.ds(PR * r, PR), :] = out.astype(jnp.bfloat16)
 
-        def conv(s_ref, w_ref, j):
-            lhs = jnp.concatenate([s_ref[dx, pl.ds(dy * PR, M), :] for dy in range(3) for dx in range(3)], axis=1)
-            rhs = jnp.concatenate([w_ref[:, pl.ds(q * CH + j * LANES, LANES)] for q in range(4)], axis=1)
-            return jnp.dot(lhs, rhs, preferred_element_type=jnp.float32)
-
-        def x_phase(t):
-            for j in range(NJ):
-                bj = jnp.concatenate([bias[pl.ds(q * CH + j * LANES, LANES)].reshape(1, LANES) for q in range(4)], axis=1)
-                g[j] = conv(sx.at[t], wx, j) + bj
-
-        def h_phase(t, last):
+        def gate_lanes(w_ref, rows, j):
+            return jnp.concatenate([w_ref[rows, pl.ds(q * CH + j * LANES, LANES)] for q in range(4)], axis=1)
+
+        def product(parts, j):
+            lhs = [s_ref[k % 3, pl.ds(k // 3 * PR, M), :] for s_ref, _, _, taps in parts for k in taps]
+            rhs = [gate_lanes(w_ref, pl.ds(k * n, n), j) for _, w_ref, n, taps in parts for k in taps]
+            return jnp.dot(jnp.concatenate(lhs, axis=1), jnp.concatenate(rhs, axis=0), preferred_element_type=jnp.float32)
+
+        def bias_block(j):
+            return jnp.concatenate([bias[pl.ds(q * CH + j * LANES, LANES)].reshape(1, LANES) for q in range(4)], axis=1)
+
+        ALL = tuple(range(9))
+        CENTRE = (4,)
+        OTHERS = (0, 1, 2, 3, 5, 6, 7, 8)
+
+        def post(t, last):
             for j in range(NJ):
                 lane = j * LANES
-                gates = conv(sh.at[t], wh, j) + g[j]
+                gates = product([(sh.at[t], wh, CH, OTHERS)], j) + g[j]
                 gi = sigmoid(gates[:, 0:LANES])
                 gf = sigmoid(gates[:, LANES:2 * LANES])
                 go = sigmoid(gates[:, 2 * LANES:3 * LANES])
@@ -174,24 +174,33 @@
                 for s in range(SEQ):
                     ho[t, s, :, :, pl.ds(lane, LANES)] = h4[:, s].astype(jnp.bfloat16)
                 if not last:
-                    put_tile(sh.at[t + 1], ech.at[t + 1], h_new, lane)
+                    put_rows(sh.at[t + 1], h_new, PR, pl.ds(lane, LANES))
+                    hf[j] = h_new
+                    put_edges(ech.at[t + 1], j)
 
         def fill(raw, s_ref, ec_ref, channels):
+            for r in range(H):
+                v = raw[r].astype(jnp.float32).reshape(PR, channels)
+                put_rows(s_ref, v, PR * (r + 1), slice(None))
+                for k in range(channels // LANES):
+                    hf[k, pl.ds(PR * r, PR), :] = v[:, k * LANES:(k + 1) * LANES]
             for k in range(channels // LANES):
-                lane = k * LANES
-                v = raw[:, :, :, pl.ds(lane, LANES)].astype(jnp.float32).reshape(M, LANES)
-                put_tile(s_ref, ec_ref, v, lane)
+                put_edges(ec_ref, k)
 
         for cp in xloads[0]:
             cp.wait()
         fill(rawx.at[0], sx.at[0], ecx.at[0], CX)
-        for cp in hloads:
-            cp.wait()
-        fill(rawh, sh.at[0], ech.at[0], CH)
         n_near = sum(exists(dr, dc).astype(jnp.int32) for dr, dc in SLOTS)
         pl.semaphore_wait(barrier, n_near)
         start_all(xcopies(0))
+        for cp in hloads:
+            cp.wait()
+        fill(rawh, sh.at[0], ech.at[0], CH)
         start_all(hcopies(0))
+        for cp in (bload, wxloads[0], whloads[0]):
+            cp.wait()
+        for j in range(NJ):
+            g[j] = product([(sx.at[0], wx, CX, CENTRE), (sh.at[0], wh, CH, CENTRE)], j) + bias_block(j)
         for t in range(1, T):
             for cp in xloads[t]:
                 cp.wait()
@@ -201,31 +210,33 @@
             fill(rawx.at[t], sx.at[t], ecx.at[t], CX)
             start_all(xcopies(t))
 
-        bload.wait()
-        for cp in cloads:
+        for cp in (*cloads, *wxloads[1:]):
             cp.wait()
         wait_recv_all(xcopies(0))
+        wait_send_all(xcopies(0))
         patch(sx.at[0], acx.at[0], CX)
-        wxload.wait()
-        x_phase(0)
-        whload.wait()
+        for j in range(NJ):
+            g[j] += product([(sx.at[0], wx, CX, OTHERS)], j)
+        for cp in whloads[1:]:
+            cp.wait()
 
         @pl.loop(0, T - 1)
         def _(t):
             wait_recv_all(hcopies(t))
+            wait_send_all(hcopies(t))
+            wait_recv_all(xcopies(t + 1))
+            wait_send_all(xcopies(t + 1))
             patch(sh.at[t], ach.at[t], CH)
-            h_phase(t, False)
+            post(t, False)
+            patch(sx.at[t + 1], acx.at[t + 1], CX)
             start_all(hcopies(t + 1))
-            wait_recv_all(xcopies(t + 1))
-            patch(sx.at[t + 1], acx.at[t + 1], CX)
-            x_phase(t + 1)
+            for j in range(NJ):
+                g[j] = product([(sx.at[t + 1], wx, CX, ALL), (sh.at[t + 1], wh, CH, CENTRE)], j) + bias_block(j)
 
         wait_recv_all(hcopies(T - 1))
+        wait_send_all(hcopies(T - 1))
         patch(sh.at[T - 1], ach.at[T - 1], CH)
-        h_phase(T - 1, True)
-        for t in range(T):
-            wait_send_all(xcopies(t))
-            wait_send_all(hcopies(t))
+        post(T - 1, True)
 
     return kernel
 
@@ -258,7 +269,7 @@
                 pltpu.VMEM((CH // LANES, M, 4 * LANES), f32), pltpu.VMEM((max(CH, CX) // LANES, M, LANES), f32),
                 pltpu.VMEM((T, 2, H, SEQ, CX), bf), pltpu.VMEM((T, 2, H, SEQ, CH), bf),
                 pltpu.VMEM((T, 2, H + 2, SEQ, CX), bf), pltpu.VMEM((T, 2, H + 2, SEQ, CH), bf),
-                pltpu.SemaphoreType.DMA((3,)), pltpu.SemaphoreType.DMA((T + 2, SEQ)),
+                pltpu.SemaphoreType.DMA((7,)), pltpu.SemaphoreType.DMA((T + 2, SEQ)),
                 pltpu.SemaphoreType.DMA((T, 8)), pltpu.SemaphoreType.DMA((T, 8)),
                 pltpu.SemaphoreType.DMA((T, 8)), pltpu.SemaphoreType.DMA((T, 8)),
             ],

time: 43.9 us -> 42 us (0.957)
  Pallas kernels: 43.2 us -> 41.2 us
    pallas_call x1, Pallas kernels: 42 us -> 40 us  [local_run(): pl.pallas_call(kernel, out_shape=(pltpu.VMEM((T, SEQ, H, W, CH), bf), plt...]
where the time goes in v3:
time: 42 us; the launch traced here: 41.9 us
  Pallas kernels  41.2 us (98%)
  between operations  0.64 us (2%)
    pallas_call x1, Pallas kernels, local_run(): pl.pallas_call(kernel, out_shape=(pltpu.VMEM((T, SEQ, H, W, CH), bf), plt...  40 us
    pallas_call x1, Pallas kernels, local_run(): pl.pallas_call(write_out, out_shape=(jax.ShapeDtypeStruct((T, SEQ, H, W,...  1.23 us

profile of v3, /device:TPU:97, one launch (start us, length us, event | category | flops | bytes accessed | tf_op | source)
XLA Modules:
  0.0 41.9 jit_solution(8420136172320624519)
XLA Ops:
  0.6 40.0 %shard_map.77 = (bf16[4,2,8,24,384]{4,3,2,1,0:T(8,128)(2,1)S(1)}, f32[8,2,24,384]{3,2,1,0:T(8,128)S(1)}) custom-call(bf16[4,2,8,24,256]{4,3,2,1,0:T(8,128)(2,1)} %frames.1, bf16[2304,1536]{1,0:T(8,128)(2,1)} %bitcast.3, bf16[3456,1536]{1,0:T(8,128)(2,1)} %bitcast.2, f32[1536]{0:T(1024)} %bias_hbm.1, bf16[2,8,24,384]{3,2,1,0:T(8,128)(2,1)} %h_init.1, ...), custom_call_target="tpu_custom_call" | custom-call | tf_op jit(solution)/shard_map/pallas_call | solution.py:260
  40.7 1.2 %shard_map.78 = (bf16[4,2,8,24,384]{4,3,2,1,0:T(8,128)(2,1)}, f32[2,8,24,384]{3,2,1,0:T(8,128)}) custom-call(bf16[4,2,8,24,384]{4,3,2,1,0:T(8,128)(2,1)S(1)} %get-tuple-element.4.h_ref, f32[8,2,24,384]{3,2,1,0:T(8,128)S(1)} %get-tuple-element.5.c_ref), custom_call_target="tpu_custom_call" | custom-call | tf_op jit(solution)/shard_map/pallas_call | solution.py:288

commit v4 on v3

--- a/solution.py
+++ b/solution.py
@@ -22,7 +22,7 @@
 
     def kernel(frames, wx_hbm, wh_hbm, bias_hbm, h_init, c_init, ho, cst,
                wx, wh, bias, rawx, rawh, sx, sh, g, hf, ecx, ech, acx, ach,
-               wsem, rsem, xsend, xrecv, hsend, hrecv):
+               wsem, rsem, send, recv):
         b = lax.axis_index("batch")
         row = lax.axis_index("rows")
         col = lax.axis_index("cols")
@@ -63,20 +63,20 @@
         zero(col == 0, [acx.at[:, 0], ach.at[:, 0]])
         zero(col == col_count - 1, [acx.at[:, 1], ach.at[:, 1]])
 
-        def copies(s_t, ec_t, ac_t, send, recv):
-            s0 = s_t.at[1]
-            parts = ((s0.at[pl.ds(M, PR)], s0.at[pl.ds(0, PR)]),
-                     (s0.at[pl.ds(PR, PR)], s0.at[pl.ds(M + PR, PR)]),
-                     (ec_t.at[1], ac_t.at[0, pl.ds(1, H)]),
-                     (ec_t.at[0], ac_t.at[1, pl.ds(1, H)]),
-                     (ec_t.at[1, H - 1], ac_t.at[0, 0]),
-                     (ec_t.at[0, H - 1], ac_t.at[1, 0]),
-                     (ec_t.at[1, 0], ac_t.at[0, H + 1]),
-                     (ec_t.at[0, 0], ac_t.at[1, H + 1]))
+        def copies(lead, s_all, ec_all, ac_all, sem_set):
+            parts = ((s_all.at[lead, 1, pl.ds(M, PR)], s_all.at[lead, 1, pl.ds(0, PR)]),
+                     (s_all.at[lead, 1, pl.ds(PR, PR)], s_all.at[lead, 1, pl.ds(M + PR, PR)]),
+                     (ec_all.at[lead, 1], ac_all.at[lead, 0, pl.ds(1, H)]),
+                     (ec_all.at[lead, 0], ac_all.at[lead, 1, pl.ds(1, H)]),
+                     (ec_all.at[lead, 1, H - 1], ac_all.at[lead, 0, 0]),
+                     (ec_all.at[lead, 0, H - 1], ac_all.at[lead, 1, 0]),
+                     (ec_all.at[lead, 1, 0], ac_all.at[lead, 0, H + 1]),
+                     (ec_all.at[lead, 0, 0], ac_all.at[lead, 1, H + 1]))
             out = []
             for i, (dr, dc) in enumerate(SLOTS):
                 cp = pltpu.make_async_remote_copy(
-                    src_ref=parts[i][0], dst_ref=parts[i][1], send_sem=send.at[i], recv_sem=recv.at[i],
+                    src_ref=parts[i][0], dst_ref=parts[i][1],
+                    send_sem=send.at[sem_set, i], recv_sem=recv.at[sem_set, i],
                     device_id=(b, col - dc, row - dr), device_id_type=MESH)
                 out.append((exists(-dr, -dc), exists(dr, dc), cp))
             return out
@@ -99,11 +99,14 @@
                 def _():
                     cp.wait_send()
 
-        def xcopies(t):
-            return copies(sx.at[t], ecx.at[t], acx.at[t], xsend.at[t], xrecv.at[t])
+        def x_first():
+            return copies(0, sx, ecx, acx, 2)
+
+        def x_rest():
+            return copies(pl.ds(1, T - 1), sx, ecx, acx, 3)
 
         def hcopies(t):
-            return copies(sh.at[t], ech.at[t], ach.at[t], hsend.at[t], hrecv.at[t])
+            return copies(t, sh, ech, ach, lax.rem(t, 3))
 
         def shifted(v):
             n, channels = v.shape
@@ -146,37 +149,47 @@
         def gate_lanes(w_ref, rows, j):
             return jnp.concatenate([w_ref[rows, pl.ds(q * CH + j * LANES, LANES)] for q in range(4)], axis=1)
 
-        def product(parts, j):
-            lhs = [s_ref[k % 3, pl.ds(k // 3 * PR, M), :] for s_ref, _, _, taps in parts for k in taps]
+        def product(parts, j, first_row=0, rows=H):
+            lhs = [s_ref[k % 3, pl.ds((k // 3 + first_row) * PR, rows * PR), :] for s_ref, _, _, taps in parts for k in taps]
             rhs = [gate_lanes(w_ref, pl.ds(k * n, n), j) for _, w_ref, n, taps in parts for k in taps]
             return jnp.dot(jnp.concatenate(lhs, axis=1), jnp.concatenate(rhs, axis=0), preferred_element_type=jnp.float32)
 
         def bias_block(j):
             return jnp.concatenate([bias[pl.ds(q * CH + j * LANES, LANES)].reshape(1, LANES) for q in range(4)], axis=1)
 
-        ALL = tuple(range(9))
         CENTRE = (4,)
-        OTHERS = (0, 1, 2, 3, 5, 6, 7, 8)
+        EARLY = (1, 7, 0)
+        LATE = (3, 6, 2, 5, 8)
+
+        def cell(t, j, gates, first_row, rows, last):
+            lanes = pl.ds(j * LANES, LANES)
+            grid_rows = pl.ds(first_row, rows)
+            gi = sigmoid(gates[:, 0:LANES])
+            gf = sigmoid(gates[:, LANES:2 * LANES])
+            go = sigmoid(gates[:, 2 * LANES:3 * LANES])
+            gg = jnp.tanh(gates[:, 3 * LANES:])
+            c_old = cst[grid_rows, :, :, lanes].reshape(rows * PR, LANES)
+            c_new = gf * c_old + gi * gg
+            cst[grid_rows, :, :, lanes] = c_new.reshape(rows, SEQ, W, LANES)
+            h_new = go * jnp.tanh(c_new)
+            h4 = h_new.reshape(rows, SEQ, W, LANES)
+            for s in range(SEQ):
+                ho[t, s, grid_rows, :, lanes] = h4[:, s].astype(jnp.bfloat16)
+            if not last:
+                put_rows(sh.at[t + 1], h_new, PR, lanes)
+                hf[j] = h_new
+                put_edges(ech.at[t + 1], j)
 
         def post(t, last):
             for j in range(NJ):
-                lane = j * LANES
-                gates = product([(sh.at[t], wh, CH, OTHERS)], j) + g[j]
-                gi = sigmoid(gates[:, 0:LANES])
-                gf = sigmoid(gates[:, LANES:2 * LANES])
-                go = sigmoid(gates[:, 2 * LANES:3 * LANES])
-                gg = jnp.tanh(gates[:, 3 * LANES:])
-                c_old = cst[:, :, :, pl.ds(lane, LANES)].reshape(M, LANES)
-                c_new = gf * c_old + gi * gg
-                cst[:, :, :, pl.ds(lane, LANES)] = c_new.reshape(H, SEQ, W, LANES)
-                h_new = go * jnp.tanh(c_new)
-                h4 = h_new.reshape(H, SEQ, W, LANES)
-                for s in range(SEQ):
-                    ho[t, s, :, :, pl.ds(lane, LANES)] = h4[:, s].astype(jnp.bfloat16)
-                if not last:
-                    put_rows(sh.at[t + 1], h_new, PR, pl.ds(lane, LANES))
-                    hf[j] = h_new
-                    put_edges(ech.at[t + 1], j)
+                halves = 2 if last and j == NJ - 1 else 1
+                rows = H // halves
+                for half in range(halves):
+                    first = half * rows
+                    gates = product([(sh.at[t], wh, CH, EARLY + LATE)], j, first, rows) + g[t, j, pl.ds(first * PR, rows * PR), :]
+                    if not last and j == NJ - 1:
+                        g[t + 1, 0] += product([(sx.at[t + 1], wx, CX, EARLY)], 0)
+                    cell(t, j, gates, first, rows, last)
 
         def fill(raw, s_ref, ec_ref, channels):
             for r in range(H):
@@ -192,46 +205,45 @@
         fill(rawx.at[0], sx.at[0], ecx.at[0], CX)
         n_near = sum(exists(dr, dc).astype(jnp.int32) for dr, dc in SLOTS)
         pl.semaphore_wait(barrier, n_near)
-        start_all(xcopies(0))
+        start_all(x_first())
         for cp in hloads:
             cp.wait()
         fill(rawh, sh.at[0], ech.at[0], CH)
         start_all(hcopies(0))
-        for cp in (bload, wxloads[0], whloads[0]):
+        for cp in (bload, wxloads[0], whloads[0], *later):
             cp.wait()
         for j in range(NJ):
-            g[j] = product([(sx.at[0], wx, CX, CENTRE), (sh.at[0], wh, CH, CENTRE)], j) + bias_block(j)
+            g[0, j] = product([(sx.at[0], wx, CX, CENTRE), (sh.at[0], wh, CH, CENTRE)], j) + bias_block(j)
         for t in range(1, T):
-            for cp in xloads[t]:
-                cp.wait()
-
-        @pl.loop(1, T)
-        def _(t):
             fill(rawx.at[t], sx.at[t], ecx.at[t], CX)
-            start_all(xcopies(t))
+        start_all(x_rest())
+        for t in range(1, T):
+            for j in range(NJ):
+                g[t, j] = product([(sx.at[t], wx, CX, CENTRE)], j) + bias_block(j)
 
         for cp in (*cloads, *wxloads[1:]):
             cp.wait()
-        wait_recv_all(xcopies(0))
-        wait_send_all(xcopies(0))
+        wait_recv_all(x_first())
+        wait_send_all(x_first())
         patch(sx.at[0], acx.at[0], CX)
         for j in range(NJ):
-            g[j] += product([(sx.at[0], wx, CX, OTHERS)], j)
+            g[0, j] += product([(sx.at[0], wx, CX, EARLY + LATE)], j)
         for cp in whloads[1:]:
             cp.wait()
+        wait_recv_all(x_rest())
+        wait_send_all(x_rest())
 
         @pl.loop(0, T - 1)
         def _(t):
             wait_recv_all(hcopies(t))
             wait_send_all(hcopies(t))
-            wait_recv_all(xcopies(t + 1))
-            wait_send_all(xcopies(t + 1))
             patch(sh.at[t], ach.at[t], CH)
+            patch(sx.at[t + 1], acx.at[t + 1], CX)
             post(t, False)
-            patch(sx.at[t + 1], acx.at[t + 1], CX)
             start_all(hcopies(t + 1))
             for j in range(NJ):
-                g[j] = product([(sx.at[t + 1], wx, CX, ALL), (sh.at[t + 1], wh, CH, CENTRE)], j) + bias_block(j)
+                x_taps = LATE if j == 0 else EARLY + LATE
+                g[t + 1, j] += product([(sx.at[t + 1], wx, CX, x_taps), (sh.at[t + 1], wh, CH, CENTRE)], j)
 
         wait_recv_all(hcopies(T - 1))
         wait_send_all(hcopies(T - 1))
@@ -266,12 +278,11 @@
                 pltpu.VMEM((9 * CX, NG), bf), pltpu.VMEM((9 * CH, NG), bf), pltpu.VMEM((NG,), f32),
                 pltpu.VMEM((T, H, SEQ, W, CX), bf), pltpu.VMEM((H, SEQ, W, CH), bf),
                 pltpu.VMEM((T, 3, M + 2 * PR, CX), bf), pltpu.VMEM((T, 3, M + 2 * PR, CH), bf),
-                pltpu.VMEM((CH // LANES, M, 4 * LANES), f32), pltpu.VMEM((max(CH, CX) // LANES, M, LANES), f32),
+                pltpu.VMEM((T, CH // LANES, M, 4 * LANES), f32), pltpu.VMEM((max(CH, CX) // LANES, M, LANES), f32),
                 pltpu.VMEM((T, 2, H, SEQ, CX), bf), pltpu.VMEM((T, 2, H, SEQ, CH), bf),
                 pltpu.VMEM((T, 2, H + 2, SEQ, CX), bf), pltpu.VMEM((T, 2, H + 2, SEQ, CH), bf),
                 pltpu.SemaphoreType.DMA((7,)), pltpu.SemaphoreType.DMA((T + 2, SEQ)),
-                pltpu.SemaphoreType.DMA((T, 8)), pltpu.SemaphoreType.DMA((T, 8)),
-                pltpu.SemaphoreType.DMA((T, 8)), pltpu.SemaphoreType.DMA((T, 8)),
+                pltpu.SemaphoreType.DMA((4, 8)), pltpu.SemaphoreType.DMA((4, 8)),
             ],
             compiler_params=pltpu.CompilerParams(
                 collective_id=0, has_side_effects=True, vmem_limit_bytes=56 * 1024 * 1024),

time: 42 us -> 41.5 us (0.988)
  Pallas kernels: 41.2 us -> 40.7 us
    pallas_call x1, Pallas kernels: 40 us -> 39.5 us  [local_run(): pl.pallas_call(kernel, out_shape=(pltpu.VMEM((T, SEQ, H, W, CH), bf), plt...]
where the time goes in v4:
time: 41.5 us; the launch traced here: 41.4 us
  Pallas kernels  40.7 us (98%)
  between operations  0.64 us (2%)
    pallas_call x1, Pallas kernels, local_run(): pl.pallas_call(kernel, out_shape=(pltpu.VMEM((T, SEQ, H, W, CH), bf), plt...  39.5 us
    pallas_call x1, Pallas kernels, local_run(): pl.pallas_call(write_out, out_shape=(jax.ShapeDtypeStruct((T, SEQ, H, W,...  1.23 us

profile of v4, /device:TPU:97, one launch (start us, length us, event | category | flops | bytes accessed | tf_op | source)
XLA Modules:
  0.0 41.4 jit_solution(16621394895895653994)
XLA Ops:
  0.6 39.5 %shard_map.77 = (bf16[4,2,8,24,384]{4,3,2,1,0:T(8,128)(2,1)S(1)}, f32[8,2,24,384]{3,2,1,0:T(8,128)S(1)}) custom-call(bf16[4,2,8,24,256]{4,3,2,1,0:T(8,128)(2,1)} %frames.1, bf16[2304,1536]{1,0:T(8,128)(2,1)} %bitcast.3, bf16[3456,1536]{1,0:T(8,128)(2,1)} %bitcast.2, f32[1536]{0:T(1024)} %bias_hbm.1, bf16[2,8,24,384]{3,2,1,0:T(8,128)(2,1)} %h_init.1, ...), custom_call_target="tpu_custom_call" | custom-call | tf_op jit(solution)/shard_map/pallas_call | solution.py:272
  40.2 1.2 %shard_map.78 = (bf16[4,2,8,24,384]{4,3,2,1,0:T(8,128)(2,1)}, f32[2,8,24,384]{3,2,1,0:T(8,128)}) custom-call(bf16[4,2,8,24,384]{4,3,2,1,0:T(8,128)(2,1)S(1)} %get-tuple-element.4.h_ref, f32[8,2,24,384]{3,2,1,0:T(8,128)S(1)} %get-tuple-element.5.c_ref), custom_call_target="tpu_custom_call" | custom-call | tf_op jit(solution)/shard_map/pallas_call | solution.py:299
